TPU v7x, 32 devices: a whole 2x2x4 slice. The times are simulated.
32 devices in a mesh: row: 8 (over z, core), col: 4 (over y, x).
Axes of the slice: x: 2, y: 2, z: 4, core: 2. Of those that a mesh axis runs over, the one named last changes fastest.
Arguments:
- basis: float32 [8192, 1024], P('row', 'col'), may hold values from -6 to 6
- merge_coef: float32 [1024, 4096], P('row', 'col'), may hold values from -0.1875 to 0.1875
- panels: float32 [2, 8192, 256], P(None, ('row', 'col')), may hold values from -0.0625 to 0.0625
- factors: float32 [2, 256, 256], replicated, may hold values from -1 to 1
Outputs:
- vectors: float32 [8192, 4096], P(('row', 'col'))
- wsum: float32 [2, 256], replicated
All inputs are finite; a program needn't handle non-finite values.
Results may differ from a plain program's by a relative error of at most 0.0001.
Values sent between devices are 32-bit elements; how exact they have to be, the bound alone decides.
No kernel may reach another device: no remote copies, remote signals or barrier semaphores. Data moves between devices by JAX's collectives and lax.ppermute only.
A program may use at most 128 MiB of HBM per device.

v0:
```python
import jax
import jax.numpy as jnp
from jax import lax
from jax.sharding import PartitionSpec as P

HI = lax.Precision.HIGHEST


def matmul(left, right):
    return jnp.dot(left, right, precision=HI, preferred_element_type=jnp.float32)


def to_tall(block):
    return lax.all_to_all(block, "col", split_axis=0, concat_axis=1, tiled=True)


def per_device(basis, merge_coef, panels, factors):
    coef = lax.all_gather(merge_coef, "row", axis=0, tiled=True)
    block = matmul(lax.all_gather(basis, "col", axis=1, tiled=True), coef)
    upper = jnp.triu(factors)
    local_v = lax.all_gather(panels, "col", axis=1, tiled=True)

    def reduce_terms(terms):
        return lax.psum(terms, "row")

    field = block
    first = local_v[0]
    second = local_v[1]
    proj_one = reduce_terms(matmul(first.T, field))
    field = field - matmul(first, matmul(upper[0], proj_one))
    proj_two = reduce_terms(matmul(second.T, field))
    field = field - matmul(second, matmul(upper[1], proj_two))
    row_one = jnp.sum(proj_one, axis=1)
    row_two = jnp.sum(proj_two, axis=1)
    row_one, row_two = lax.psum((row_one, row_two), "col")
    field = to_tall(field)
    scale = jnp.sqrt(jnp.float32(field.shape[1]))
    return (field, jnp.stack([row_one, row_two]) / scale)


def solution(mesh):
    placed = (P("row", "col"), P("row", "col"), P(None, ("row", "col"), None), P())
    return jax.shard_map(
        per_device,
        mesh=mesh,
        in_specs=placed,
        out_specs=(P(("row", "col"), None), P()),
        check_vma=False,
    )
```

profile of v0, /device:TPU:0, one launch (start us, length us, event | category | flops | bytes accessed | tf_op | source)
XLA Modules:
  0.0 370.3 jit_solution(15266776425502628769)
XLA Ops:
  7.2 0.7 all-gather.4.cloned.1.call-update
  7.9 0.7 all-gather.6.cloned.1.call-update
  8.7 0.7 all-gather.8.cloned.1.call-update
  9.4 55.6 %all-gather.4.cloned.1.call-done = f32[1024,1024]{1,0:T(8,128)} async-done(((f32[1024,256]{1,0:T(8,128)}), f32[1024,1024]{1,0:T(8,128)}) %all-gather.4.cloned.1.call-update) | async-done | bytes 4194320 | tf_op jit(solution)/shard_map/all_gather | solution.py:19
  65.0 48.5 %all-gather.6.cloned.1.call-done = f32[1024,1024]{1,0:T(8,128)} async-done(((f32[128,1024]{1,0:T(8,128)}), f32[1024,1024]{1,0:T(8,128)}) %all-gather.6.cloned.1.call-update) | async-done | bytes 4194320 | tf_op jit(solution)/shard_map/all_gather | solution.py:18
  113.5 17.5 %fusion.2 = f32[1024,1024]{1,0:T(8,128)} fusion(f32[1024,1024]{1,0:T(8,128)} %all-gather.4.cloned.1.call-done, f32[1024,1024]{1,0:T(8,128)} %all-gather.6.cloned.1.call-done), kind=kOutput, calls=%fused_computation.14 | convolution fusion | flops 12884901888 | bytes 12582912 | tf_op jit(solution)/shard_map/dot_general | solution.py:10
  131.0 18.4 %all-gather.8.cloned.1.call-done = f32[2,1024,256]{2,1,0:T(8,128)} async-done(((f32[2,256,256]{2,1,0:T(8,128)}), f32[2,1024,256]{2,1,0:T(8,128)}) %all-gather.8.cloned.1.call-update) | async-done | bytes 2097168 | tf_op jit(solution)/shard_map/all_gather | solution.py:21
  149.4 10.3 %convolution_bitcast_fusion.1 = f32[256,1024]{0,1:T(8,128)} fusion(f32[1024,1024]{1,0:T(8,128)} %fusion.2, f32[2,1024,256]{2,1,0:T(8,128)} %all-gather.8.cloned.1.call-done), kind=kOutput, calls=%fused_computation.3 | convolution fusion | flops 3221225472 | bytes 6291456 | tf_op jit(solution)/shard_map/dot_general | solution.py:10
  159.8 0.1 iota_compare_fusion
  159.9 0.1 broadcast_select_fusion
  159.9 59.2 %all-reduce.4.cloned.1.call-done = f32[256,1024]{0,1:T(8,128)} async-done(((f32[256,1024]{0,1:T(8,128)}), f32[256,1024]{0,1:T(8,128)}) %all-reduce.4.cloned.1.call-update) | async-done | bytes 1048592 | tf_op jit(solution)/shard_map/psum | solution.py:24
  219.2 2.3 fusion.1
  221.4 5.7 %bitcast_subtract_fusion.1 = f32[1024,1024]{1,0:T(8,128)S(1)} fusion(f32[1024,1024]{1,0:T(8,128)} %fusion.2, f32[256,1024]{1,0:T(8,128)S(1)} %fusion.1, f32[2,1024,256]{2,1,0:T(8,128)S(1)} %copy-done.1), kind=kOutput, calls=%fused_computation.1 | convolution fusion | flops 3222274048 | bytes 10485760 | tf_op jit(solution)/shard_map/dot_general | solution.py:10
  227.1 2.0 copy-done
  229.1 7.8 %convolution_bitcast_fusion = f32[256,1024]{0,1:T(8,128)} fusion(f32[1024,1024]{1,0:T(8,128)S(1)} %bitcast_subtract_fusion.1, f32[2,1024,256]{2,1,0:T(8,128)S(1)} %copy-done.1), kind=kOutput, calls=%fused_computation.2 | convolution fusion | flops 3221225472 | bytes 6291456 | tf_op jit(solution)/shard_map/dot_general | solution.py:10
  237.0 58.5 %all-reduce.6.cloned.1.call-done = f32[256,1024]{0,1:T(8,128)} async-done(((f32[256,1024]{0,1:T(8,128)}), f32[256,1024]{0,1:T(8,128)}) %all-reduce.6.cloned.1.call-update) | async-done | bytes 1048592 | tf_op jit(solution)/shard_map/psum | solution.py:24
  295.5 2.3 fusion
  297.7 6.7 %bitcast_subtract_fusion = f32[1024,1024]{1,0:T(8,128)} fusion(f32[1024,1024]{1,0:T(8,128)} %copy-done, f32[256,1024]{1,0:T(8,128)S(1)} %fusion, f32[2,1024,256]{2,1,0:T(8,128)S(1)} %copy-done.1), kind=kOutput, calls=%fused_computation | convolution fusion | flops 3222274048 | bytes 10485760 | tf_op jit(solution)/shard_map/dot_general | solution.py:10
  304.4 5.0 %all-to-all-start = ((f32[4,256,1024]{2,1,0:T(8,128)}), f32[4,256,1024]{2,1,0:T(8,128)}, u32[]{:S(2)}, u32[]{:S(2)}) async-start(f32[4,256,1024]{2,1,0:T(8,128)} %bitcast.36), calls=%async_computation | async-start | bytes 8388608 | tf_op jit(solution)/shard_map/all_to_all | solution.py:14
  309.4 0.2 reduce_sum.18
  309.6 0.2 reduce_sum.19
  309.7 48.7 %all-reduce = (f32[1,256]{1,0:T(1,128)S(1)}, f32[1,256]{1,0:T(1,128)S(1)}) all-reduce(f32[1,256]{1,0:T(1,128)S(1)} %bitcast.39, f32[1,256]{1,0:T(1,128)S(1)} %bitcast.38), channel_id=1, replica_groups=mesh['row'=8,'col'=4] {'col'}, use_global_device_ids=true, to_apply=%region_5.6 | all-reduce | flops 512 | bytes 4096 | tf_op jit(solution)/shard_map/psum | solution.py:35
  358.4 0.6 maximum_multiply_fusion
  359.0 4.8 %copy.7 = f32[4,32,8,1024]{3,2,0,1:T(8,128)} copy(f32[4,32,8,1024]{3,2,1,0:T(8,128)} %bitcast.12) | data formatting | bytes 8388608 | tf_op jit(solution)/shard_map/all_to_all | solution.py:14
  (18 shorter events, 0.3 us)
Async XLA Ops:
  7.2 57.8 %all-gather.4.cloned.1.call-start = ((), (), s32[]{:S(2)}) async-start(), calls=%async_computation.1 | async-start | bytes 5242880 | tf_op jit(solution)/shard_map/all_gather | solution.py:19
  7.9 105.6 %all-gather.6.cloned.1.call-start = ((), (), s32[]{:S(2)}) async-start(), calls=%async_computation.2 | async-start | bytes 4718592 | tf_op jit(solution)/shard_map/all_gather | solution.py:18
  8.6 140.7 %all-gather.8.cloned.1.call-start = ((), (), s32[]{:S(2)}) async-start(), calls=%async_computation.3 | async-start | bytes 2621440 | tf_op jit(solution)/shard_map/all_gather | solution.py:21
  9.4 209.8 %all-reduce.4.cloned.1.call-start = ((), (), s32[]{:S(2)}) async-start(), calls=%async_computation.4 | async-start | bytes 2097152 | tf_op jit(solution)/shard_map/psum | solution.py:24
  131.0 28.9 %copy-start.4 = (f32[2,256,256]{2,1,0:T(8,128)S(1)}, f32[2,256,256]{2,1,0:T(8,128)}, u32[]{:S(2)}) copy-start(f32[2,256,256]{2,1,0:T(8,128)} %param.7) | copy-start | bytes 1572868
  149.4 72.1 %copy-start.1 = (f32[2,1024,256]{2,1,0:T(8,128)S(1)}, f32[2,1024,256]{2,1,0:T(8,128)}, u32[]{:S(2)}) copy-start(f32[2,1024,256]{2,1,0:T(8,128)} %all-gather.8.cloned.1.call-done) | copy-start | bytes 6291460
  159.7 135.8 %all-reduce.6.cloned.1.call-start = ((), (), s32[]{:S(2)}) async-start(), calls=%async_computation.5 | async-start | bytes 2097152 | tf_op jit(solution)/shard_map/psum | solution.py:24
  227.1 2.0 copy-start
  304.4 5.0 %copy-start.2 = (f32[256,1024]{0,1:T(8,128)S(1)}, f32[256,1024]{0,1:T(8,128)}, u32[]{:S(2)}) copy-start(f32[256,1024]{0,1:T(8,128)} %all-reduce.4.cloned.1.call-done) | copy-start | bytes 3145732
  304.4 5.1 %copy-start.3 = (f32[256,1024]{0,1:T(8,128)S(1)}, f32[256,1024]{0,1:T(8,128)}, u32[]{:S(2)}) copy-start(f32[256,1024]{0,1:T(8,128)} %all-reduce.6.cloned.1.call-done) | copy-start | bytes 3145732
  304.4 54.5 %all-to-all-start = ((f32[4,256,1024]{2,1,0:T(8,128)}), f32[4,256,1024]{2,1,0:T(8,128)}, u32[]{:S(2)}, u32[]{:S(2)}) async-start(f32[4,256,1024]{2,1,0:T(8,128)} %bitcast.36), calls=%async_computation | async-start | bytes 8388608 | tf_op jit(solution)/shard_map/all_to_all | solution.py:14
Sparse Core Ops, SparseCore 0:
  9.8 55.1 all-gather.3
  66.6 46.8 all-gather.5
  115.3 33.9 all-gather.7
  159.8 59.2 all-reduce.3
  237.1 58.2 all-reduce.5
where the time goes:
time: 371 us; the launch traced here: 370 us
  waiting for transfers between devices  242 us (65%)
  matrix products  52.5 us (14%)
  blocking collectives  48.7 us (13%)
  between operations  13.9 us (4%)
  local copies, waits for them, and re-layouts  6.81 us (2%)
  starting transfers between devices  5.16 us (1%)
    psum x2, waiting for transfers between devices, reduce_terms(): return lax.psum(terms, 'row')  118 us
    all_gather x1, waiting for transfers between devices, per_device(): block = matmul(lax.all_gather(basis, 'col', axis=1, tiled=True), coef)  55.6 us
    dot_general x7, matrix products, matmul(): jnp.dot(left, right, precision=HI, preferred_element_type=jnp.float32)  52.5 us
    psum x1, blocking collectives, per_device(): row_one, row_two = lax.psum((row_one, row_two), 'col')  48.7 us
    all_gather x1, waiting for transfers between devices, per_device(): coef = lax.all_gather(merge_coef, 'row', axis=0, tiled=True)  48.5 us
    all_gather x1, waiting for transfers between devices, per_device(): local_v = lax.all_gather(panels, 'col', axis=1, tiled=True)  18.4 us
  transfers between devices with their start and end apart: 6, of which 5 were waited for; matrix products, arithmetic and copies ran while one was open for 5% of the time, Pallas kernels for 0%

commit v1 on v0

--- a/solution.py
+++ b/solution.py
@@ -2,6 +2,7 @@
 import jax.numpy as jnp
 from jax import lax
 from jax.sharding import PartitionSpec as P
+from jax.lax import axis_index, ppermute, psum
 
 HI = lax.Precision.HIGHEST
 
@@ -15,7 +16,15 @@
 
 
 def per_device(basis, merge_coef, panels, factors):
-    coef = lax.all_gather(merge_coef, "row", axis=0, tiled=True)
+    chips = psum(1, "row")
+    answer = sorted(((num, (num + 1) % chips) for num in range(chips)))
+    left_arr = merge_coef
+    log = [left_arr]
+    for kk in range(1, chips):
+        left_arr = ppermute(left_arr, axis_name="row", perm=answer)
+        log.insert(0, left_arr)
+    heard = jnp.concatenate(log, 0)
+    coef = jnp.roll(heard, (axis_index("row") + 1) * merge_coef.shape[0], 0)
     block = matmul(lax.all_gather(basis, "col", axis=1, tiled=True), coef)
     upper = jnp.triu(factors)
     local_v = lax.all_gather(panels, "col", axis=1, tiled=True)

time: 371 us -> 338 us (0.911)
  waiting for transfers between devices: 242 us -> 191 us
  local copies, waits for them, and re-layouts: 6.81 us -> 24.5 us
    ppermute x0 -> x7, waiting for transfers between devices: none -> 73.9 us  [per_device(): left_arr = ppermute(left_arr, axis_name='row', perm=answer)]
    all_gather x1, waiting for transfers between devices: 55.6 us -> 0.01 us  [per_device(): block = matmul(lax.all_gather(basis, 'col', axis=1, tiled=True), coef)]
    all_gather x1 -> x0, waiting for transfers between devices: 48.5 us -> none  [per_device(): coef = lax.all_gather(merge_coef, 'row', axis=0, tiled=True)]
    all_gather x1, waiting for transfers between devices: 18.4 us -> 0.01 us  [per_device(): local_v = lax.all_gather(panels, 'col', axis=1, tiled=True)]
    unnamed x10 -> x27, local copies, waits for them, and re-layouts: 2.02 us -> 18.8 us
  transfers between devices with their start and end apart: 6 -> 12, of which waited for: 5 -> 9; matrix products, arithmetic and copies ran while one was open for 5% -> 11% of each run, Pallas kernels for 0% -> 0%
where the time goes in v1:
time: 338 us
  waiting for transfers between devices  191 us (57%)
  matrix products  52.9 us (16%)
  blocking collectives  48.7 us (14%)
  local copies, waits for them, and re-layouts  24.5 us (7%)
  between operations  13.9 us (4%)
  starting transfers between devices  5.69 us (2%)
    psum x2, waiting for transfers between devices, reduce_terms(): return lax.psum(terms, 'row')  116 us
    ppermute x7, waiting for transfers between devices, per_device(): left_arr = ppermute(left_arr, axis_name='row', perm=answer)  73.9 us
    dot_general x7, matrix products, matmul(): jnp.dot(left, right, precision=HI, preferred_element_type=jnp.float32)  52.9 us
    psum x1, blocking collectives, per_device(): row_one, row_two = lax.psum((row_one, row_two), 'col')  48.7 us
    unnamed x27, local copies, waits for them, and re-layouts  18.8 us
  transfers between devices with their start and end apart: 12, of which 9 were waited for; matrix products, arithmetic and copies ran while one was open for 11% of the time, Pallas kernels for 0%

profile of v1, /device:TPU:0, one launch (start us, length us, event | category | flops | bytes accessed | tf_op | source)
XLA Modules:
  0.0 337.7 jit_solution(13808988333008963320)
XLA Ops:
  8.5 11.1 %collective-permute-done = f32[128,1024]{1,0:T(8,128)S(1)} collective-permute-done((f32[128,1024]{1,0:T(8,128)}, f32[128,1024]{1,0:T(8,128)S(1)}, u32[]{:S(2)}, u32[]{:S(2)}) %collective-permute-start) | collective-permute-done | bytes 524320 | tf_op jit(solution)/shard_map/ppermute | solution.py:24
  19.6 10.4 %collective-permute-done.1 = f32[128,1024]{1,0:T(8,128)S(1)} collective-permute-done((f32[128,1024]{1,0:T(8,128)S(1)}, f32[128,1024]{1,0:T(8,128)S(1)}, u32[]{:S(2)}, u32[]{:S(2)}) %collective-permute-start.1) | collective-permute-done | bytes 524320 | tf_op jit(solution)/shard_map/ppermute | solution.py:24
  30.0 10.4 %collective-permute-done.2 = f32[128,1024]{1,0:T(8,128)S(1)} collective-permute-done((f32[128,1024]{1,0:T(8,128)S(1)}, f32[128,1024]{1,0:T(8,128)S(1)}, u32[]{:S(2)}, u32[]{:S(2)}) %collective-permute-start.2) | collective-permute-done | bytes 524320 | tf_op jit(solution)/shard_map/ppermute | solution.py:24
  40.4 10.4 %collective-permute-done.3 = f32[128,1024]{1,0:T(8,128)S(1)} collective-permute-done((f32[128,1024]{1,0:T(8,128)S(1)}, f32[128,1024]{1,0:T(8,128)S(1)}, u32[]{:S(2)}, u32[]{:S(2)}) %collective-permute-start.3) | collective-permute-done | bytes 524320 | tf_op jit(solution)/shard_map/ppermute | solution.py:24
  50.8 10.4 %collective-permute-done.4 = f32[128,1024]{1,0:T(8,128)S(1)} collective-permute-done((f32[128,1024]{1,0:T(8,128)S(1)}, f32[128,1024]{1,0:T(8,128)S(1)}, u32[]{:S(2)}, u32[]{:S(2)}) %collective-permute-start.4) | collective-permute-done | bytes 524320 | tf_op jit(solution)/shard_map/ppermute | solution.py:24
  61.3 10.4 %collective-permute-done.5 = f32[128,1024]{1,0:T(8,128)} collective-permute-done((f32[128,1024]{1,0:T(8,128)S(1)}, f32[128,1024]{1,0:T(8,128)}, u32[]{:S(2)}, u32[]{:S(2)}) %collective-permute-start.5) | collective-permute-done | bytes 524320 | tf_op jit(solution)/shard_map/ppermute | solution.py:24
  71.7 10.7 %collective-permute-done.6 = f32[128,1024]{1,0:T(8,128)} collective-permute-done((f32[128,1024]{1,0:T(8,128)}, f32[128,1024]{1,0:T(8,128)}, u32[]{:S(2)}, u32[]{:S(2)}) %collective-permute-start.6) | collective-permute-done | bytes 524320 | tf_op jit(solution)/shard_map/ppermute | solution.py:24
  82.4 1.9 constant_dynamic-update-slice_fusion.15
  84.3 1.9 constant_dynamic-update-slice_fusion.14
  91.3 1.9 constant_dynamic-update-slice_fusion.7
  93.2 1.9 constant_dynamic-update-slice_fusion.6
  100.1 17.8 %fusion = f32[1024,1024]{0,1:T(8,128)} fusion(f32[1024,1024]{1,0:T(8,128)} %all-gather.3.cloned.1.call-done, f32[2048,1024]{1,0:T(8,128)} %constant_dynamic-update-slice_fusion, s32[]{:T(128)S(6)} %select_n.18), kind=kOutput, calls=%fused_computation | convolution fusion | flops 12884901888 | bytes 12582916 | tf_op jit(solution)/shard_map/dot_general | solution.py:11
  117.9 10.3 %convolution_bitcast_fusion.1 = f32[256,1024]{0,1:T(8,128)} fusion(f32[1024,1024]{0,1:T(8,128)} %fusion, f32[2,1024,256]{2,1,0:T(8,128)} %all-gather.5.cloned.1.call-done), kind=kOutput, calls=%fused_computation.5 | convolution fusion | flops 3221225472 | bytes 6291456 | tf_op jit(solution)/shard_map/dot_general | solution.py:11
  128.4 57.9 %all-reduce.4.cloned.1.call-done = f32[256,1024]{0,1:T(8,128)} async-done(((f32[256,1024]{0,1:T(8,128)}), f32[256,1024]{0,1:T(8,128)}) %all-reduce.4.cloned.1.call-update) | async-done | bytes 1048592 | tf_op jit(solution)/shard_map/psum | solution.py:33
  186.4 2.3 fusion.3
  188.6 5.7 %convolution_subtract_fusion.1 = f32[1024,1024]{0,1:T(8,128)S(1)} fusion(f32[1024,1024]{0,1:T(8,128)} %fusion, f32[256,1024]{1,0:T(8,128)S(1)} %fusion.3, f32[2,1024,256]{2,1,0:T(8,128)S(1)} %copy-done.1), kind=kOutput, calls=%fused_computation.3 | convolution fusion | flops 3222274048 | bytes 10485760 | tf_op jit(solution)/shard_map/dot_general | solution.py:11
  194.3 2.0 copy-done
  196.3 7.8 %convolution_bitcast_fusion = f32[256,1024]{0,1:T(8,128)} fusion(f32[1024,1024]{0,1:T(8,128)S(1)} %convolution_subtract_fusion.1, f32[2,1024,256]{2,1,0:T(8,128)S(1)} %copy-done.1), kind=kOutput, calls=%fused_computation.4 | convolution fusion | flops 3221225472 | bytes 6291456 | tf_op jit(solution)/shard_map/dot_general | solution.py:11
  204.2 58.5 %all-reduce.6.cloned.1.call-done = f32[256,1024]{0,1:T(8,128)} async-done(((f32[256,1024]{0,1:T(8,128)}), f32[256,1024]{0,1:T(8,128)}) %all-reduce.6.cloned.1.call-update) | async-done | bytes 1048592 | tf_op jit(solution)/shard_map/psum | solution.py:33
  262.7 2.3 fusion.2
  265.0 6.8 %convolution_subtract_fusion = f32[1024,1024]{0,1:T(8,128)} fusion(f32[1024,1024]{0,1:T(8,128)} %copy-done, f32[256,1024]{1,0:T(8,128)S(1)} %fusion.2, f32[2,1024,256]{2,1,0:T(8,128)S(1)} %copy-done.1), kind=kOutput, calls=%fused_computation.2 | convolution fusion | flops 3222274048 | bytes 10485760 | tf_op jit(solution)/shard_map/dot_general | solution.py:11
  271.8 5.0 %all-to-all-start = ((f32[4,256,1024]{2,1,0:T(8,128)}), f32[4,256,1024]{2,1,0:T(8,128)}, u32[]{:S(2)}, u32[]{:S(2)}) async-start(f32[4,256,1024]{2,1,0:T(8,128)} %bitcast.33), calls=%async_computation | async-start | bytes 8388608 | tf_op jit(solution)/shard_map/all_to_all | solution.py:15
  277.1 48.7 %all-reduce = (f32[1,256]{1,0:T(1,128)S(1)}, f32[1,256]{1,0:T(1,128)S(1)}) all-reduce(f32[1,256]{1,0:T(1,128)S(1)} %bitcast.36, f32[1,256]{1,0:T(1,128)S(1)} %bitcast.35), channel_id=1, replica_groups=mesh['row'=8,'col'=4] {'col'}, use_global_device_ids=true, to_apply=%region_5.6 | all-reduce | flops 512 | bytes 4096 | tf_op jit(solution)/shard_map/psum | solution.py:44
  326.3 4.8 %copy.7 = f32[4,32,8,1024]{3,2,0,1:T(8,128)} copy(f32[4,32,8,1024]{3,2,1,0:T(8,128)} %bitcast.12) | data formatting | bytes 8388608 | tf_op jit(solution)/shard_map/all_to_all | solution.py:15
  (47 shorter events, 12.6 us)
Async XLA Ops:
  7.2 83.3 %copy-start.4 = (f32[128,1024]{1,0:T(8,128)S(1)}, f32[128,1024]{1,0:T(8,128)}, u32[]{:S(2)}) copy-start(f32[128,1024]{1,0:T(8,128)} %param.5) | copy-start | bytes 1572868
  7.2 92.9 %all-gather.3.cloned.1.call-start = ((), (), s32[]{:S(2)}) async-start(), calls=%async_computation.1 | async-start | bytes 5242880 | tf_op jit(solution)/shard_map/all_gather | solution.py:28
  7.9 110.0 %all-gather.5.cloned.1.call-start = ((), (), s32[]{:S(2)}) async-start(), calls=%async_computation.2 | async-start | bytes 2621440 | tf_op jit(solution)/shard_map/all_gather | solution.py:30
  8.0 11.6 %collective-permute-start = (f32[128,1024]{1,0:T(8,128)}, f32[128,1024]{1,0:T(8,128)S(1)}, u32[]{:S(2)}, u32[]{:S(2)}) collective-permute-start(f32[128,1024]{1,0:T(8,128)} %param.5), channel_id=1, source_target_pairs={{0,4},{4,8},{8,12},{12,16},{16,20},{20,24},{24,28},{28,0},{1,5},{5... | collective-permute-start | bytes 1572872 | tf_op jit(solution)/shard_map/ppermute | solution.py:24
  19.6 10.4 %collective-permute-start.1 = (f32[128,1024]{1,0:T(8,128)S(1)}, f32[128,1024]{1,0:T(8,128)S(1)}, u32[]{:S(2)}, u32[]{:S(2)}) collective-permute-start(f32[128,1024]{1,0:T(8,128)S(1)} %collective-permute-done), channel_id=1, source_target_pairs={{0,4},{4,8},{8,12},{12,16},{16,20},{20,24},{24,28},{28,0},{1,5},{5... | collective-permute-start | bytes 1572872 | tf_op jit(solution)/shard_map/ppermute | solution.py:24
  30.0 10.4 %collective-permute-start.2 = (f32[128,1024]{1,0:T(8,128)S(1)}, f32[128,1024]{1,0:T(8,128)S(1)}, u32[]{:S(2)}, u32[]{:S(2)}) collective-permute-start(f32[128,1024]{1,0:T(8,128)S(1)} %collective-permute-done.1), channel_id=1, source_target_pairs={{0,4},{4,8},{8,12},{12,16},{16,20},{20,24},{24,28},{28,0},{1,5},{5... | collective-permute-start | bytes 1572872 | tf_op jit(solution)/shard_map/ppermute | solution.py:24
  40.4 10.4 %collective-permute-start.3 = (f32[128,1024]{1,0:T(8,128)S(1)}, f32[128,1024]{1,0:T(8,128)S(1)}, u32[]{:S(2)}, u32[]{:S(2)}) collective-permute-start(f32[128,1024]{1,0:T(8,128)S(1)} %collective-permute-done.2), channel_id=1, source_target_pairs={{0,4},{4,8},{8,12},{12,16},{16,20},{20,24},{24,28},{28,0},{1,5},{5... | collective-permute-start | bytes 1572872 | tf_op jit(solution)/shard_map/ppermute | solution.py:24
  50.8 10.4 %collective-permute-start.4 = (f32[128,1024]{1,0:T(8,128)S(1)}, f32[128,1024]{1,0:T(8,128)S(1)}, u32[]{:S(2)}, u32[]{:S(2)}) collective-permute-start(f32[128,1024]{1,0:T(8,128)S(1)} %collective-permute-done.3), channel_id=1, source_target_pairs={{0,4},{4,8},{8,12},{12,16},{16,20},{20,24},{24,28},{28,0},{1,5},{5... | collective-permute-start | bytes 1572872 | tf_op jit(solution)/shard_map/ppermute | solution.py:24
  61.2 10.5 %collective-permute-start.5 = (f32[128,1024]{1,0:T(8,128)S(1)}, f32[128,1024]{1,0:T(8,128)}, u32[]{:S(2)}, u32[]{:S(2)}) collective-permute-start(f32[128,1024]{1,0:T(8,128)S(1)} %collective-permute-done.4), channel_id=1, source_target_pairs={{0,4},{4,8},{8,12},{12,16},{16,20},{20,24},{24,28},{28,0},{1,5},{5... | collective-permute-start | bytes 1572872 | tf_op jit(solution)/shard_map/ppermute | solution.py:24
  61.2 125.1 %all-reduce.4.cloned.1.call-start = ((), (), s32[]{:S(2)}) async-start(), calls=%async_computation.3 | async-start | bytes 2097152 | tf_op jit(solution)/shard_map/psum | solution.py:33
  71.7 10.7 %collective-permute-start.6 = (f32[128,1024]{1,0:T(8,128)}, f32[128,1024]{1,0:T(8,128)}, u32[]{:S(2)}, u32[]{:S(2)}) collective-permute-start(f32[128,1024]{1,0:T(8,128)} %collective-permute-done.5), channel_id=1, source_target_pairs={{0,4},{4,8},{8,12},{12,16},{16,20},{20,24},{24,28},{28,0},{1,5},{5... | collective-permute-start | bytes 1572872 | tf_op jit(solution)/shard_map/ppermute | solution.py:24
  100.1 28.3 %copy-start.5 = (f32[2,256,256]{2,1,0:T(8,128)S(1)}, f32[2,256,256]{2,1,0:T(8,128)}, u32[]{:S(2)}) copy-start(f32[2,256,256]{2,1,0:T(8,128)} %param.7) | copy-start | bytes 1572868
  117.9 70.7 %copy-start.1 = (f32[2,1024,256]{2,1,0:T(8,128)S(1)}, f32[2,1024,256]{2,1,0:T(8,128)}, u32[]{:S(2)}) copy-start(f32[2,1024,256]{2,1,0:T(8,128)} %all-gather.5.cloned.1.call-done) | copy-start | bytes 6291460
  128.2 134.6 %all-reduce.6.cloned.1.call-start = ((), (), s32[]{:S(2)}) async-start(), calls=%async_computation.4 | async-start | bytes 2097152 | tf_op jit(solution)/shard_map/psum | solution.py:33
  194.3 2.0 copy-start
  265.0 11.8 %copy-start.2 = (f32[256,1024]{0,1:T(8,128)S(1)}, f32[256,1024]{0,1:T(8,128)}, u32[]{:S(2)}) copy-start(f32[256,1024]{0,1:T(8,128)} %all-reduce.4.cloned.1.call-done) | copy-start | bytes 3145732
  271.8 5.1 %copy-start.3 = (f32[256,1024]{0,1:T(8,128)S(1)}, f32[256,1024]{0,1:T(8,128)}, u32[]{:S(2)}) copy-start(f32[256,1024]{0,1:T(8,128)} %all-reduce.6.cloned.1.call-done) | copy-start | bytes 3145732
  271.8 54.6 %all-to-all-start = ((f32[4,256,1024]{2,1,0:T(8,128)}), f32[4,256,1024]{2,1,0:T(8,128)}, u32[]{:S(2)}, u32[]{:S(2)}) async-start(f32[4,256,1024]{2,1,0:T(8,128)} %bitcast.33), calls=%async_computation | async-start | bytes 8388608 | tf_op jit(solution)/shard_map/all_to_all | solution.py:15
Sparse Core Ops, SparseCore 0:
  9.8 55.1 all-gather.2
  66.8 35.1 all-gather.4
  128.3 58.0 all-reduce.3
  204.3 58.3 all-reduce.5
